TPU v7x, 128 devices: a whole 4x4x4 slice. The times are simulated.
128 devices in a mesh: ep: 32 (over z, x, core), dp: 4 (over y).
Axes of the slice: x: 4, y: 4, z: 4, core: 2. Of those that a mesh axis runs over, the one named last changes fastest.
Arguments:
- grad_out: float32 [16384, 1536], P(('ep', 'dp')), may hold values from -6 to 6
- tokens: bfloat16 [16384, 1536], P(('ep', 'dp')), may hold values from -6 to 6
- probs: float32 [16384, 4], P(('ep', 'dp')), may hold values from 0.1 to 0.5
- expert_ids: int32 [16384, 4], P(('ep', 'dp')), may hold values from 0 to 31, all different within a row; in each aligned block of 128 rows (0 to 127, 128 to 255, ...) at most 20 rows name the same one
- priority: int32 [128, 128], P(('ep', 'dp')), may hold values from 0 to 127, each once within a row
- cap_counts: int32 [32], replicated, may hold values from 10 to 20, as said below
- gate_weight: bfloat16 [32, 1536, 1536], P('ep'), may hold values from -0.15625 to 0.15625
- up_weight: bfloat16 [32, 1536, 1536], P('ep'), may hold values from -0.15625 to 0.15625
- down_weight: bfloat16 [32, 1536, 1536], P('ep'), may hold values from -0.15625 to 0.15625
Outputs:
- input_grad: bfloat16 [16384, 1536], P(('ep', 'dp'))
- prob_grad: float32 [16384, 4], P(('ep', 'dp'))
- gate_grad: bfloat16 [32, 1536, 1536], P('ep', 'dp')
- up_grad: bfloat16 [32, 1536, 1536], P('ep', 'dp')
- down_grad: bfloat16 [32, 1536, 1536], P('ep', 'dp')
Inputs may be any that keep to these rules, and one draw needn't show every extreme that they name: `expert_ids`: each row names 4 different experts; among the rows of one device no expert is named by more than 20 rows, and in some device some expert is named by exactly 20 rows. `priority`: each row orders the 128 tokens of one device, each number once. `cap_counts`: some expert has exactly 20.
All inputs are finite; a program needn't handle non-finite values. Where the computation divides by a largest or mean magnitude, that divisor is 1e-20 or more.
Results may differ from a plain program's by a relative error of at most 0.017.
Values may be sent and summed in bfloat16 or wider, within the bound.
A program may use at most 128 MiB of HBM per device.

v0:
```python
import jax
import jax.numpy as jnp
from jax import lax
from jax.sharding import PartitionSpec as P

sharpness = 1.702


def contract_last(first_op, second_op):
    return lax.dot_general(
        first_op, second_op, (((1,), (1,)), ((), ())), preferred_element_type=jnp.float32
    )


def contract_first(first_op, second_op):
    return lax.dot_general(
        first_op, second_op, (((0,), (0,)), ((), ())), preferred_element_type=jnp.float32
    )


def route_table(expert_ids, priority, cap_counts, buckets, capacity):
    ranking = priority[0]
    earlier = (ranking[None, :] < ranking[:, None]).astype(jnp.float32)
    expert_range = lax.broadcasted_iota(jnp.int32, (1, 1, buckets), 2)
    matches = (expert_ids[:, :, None] == expert_range).astype(jnp.float32)
    routed = jnp.sum(matches, axis=1)
    before = jnp.dot(earlier, routed)
    slot_rank = jnp.sum(matches * before[:, None, :], axis=2)
    keep_limit = jnp.sum(matches * cap_counts.astype(jnp.float32)[None, None, :], axis=2)
    slot_range = lax.broadcasted_iota(jnp.float32, (1, 1, capacity), 2)
    slot_hit = (
        (slot_rank[:, :, None] == slot_range) & (slot_rank < keep_limit)[:, :, None]
    ).astype(jnp.float32)
    placement = matches[:, :, :, None] * slot_hit[:, :, None, :]
    return placement.reshape(expert_ids.shape[0], expert_ids.shape[1], buckets * capacity)


def deltas(slot_x, slot_g, w_gate, w_up, w_down):
    gate_pre = contract_last(slot_x, w_gate)
    up_pre = contract_last(slot_x, w_up)
    act_delta = contract_last(slot_g, w_down)
    squash = jax.nn.sigmoid(sharpness * gate_pre)
    gated = gate_pre * squash
    activated = (up_pre + 1.0) * gated
    up_delta = (act_delta * gated).astype(jnp.bfloat16)
    gate_delta = (
        act_delta * (up_pre + 1.0) * (squash + sharpness * gate_pre * squash * (1.0 - squash))
    ).astype(jnp.bfloat16)
    return (activated, act_delta, gate_delta, up_delta)


def on_device(
    grad_out, tokens, probs, expert_ids, priority, cap_counts, gate_weight, up_weight, down_weight
):
    ep_size = lax.axis_size("ep")
    dp_size = lax.axis_size("dp")
    tok_rows, model_width = tokens.shape
    route_count = expert_ids.shape[1]
    capacity = 5 * route_count * tok_rows // (4 * ep_size)
    slot_rows = ep_size * capacity
    placement = route_table(expert_ids, priority, cap_counts, ep_size, capacity)
    slot_table = jnp.sum(placement, axis=1)
    table_low = slot_table.astype(jnp.bfloat16)
    row_scale = jnp.maximum(jnp.max(jnp.abs(grad_out), axis=1), 1.0)
    quantized = (grad_out / row_scale[:, None]).astype(jnp.bfloat16)
    send_prob = jnp.sum(placement * probs[:, :, None], axis=(0, 1))
    send_scale = jnp.sum(slot_table * row_scale[:, None], axis=0)
    send_x = jnp.einsum("ts,td->sd", table_low, tokens, preferred_element_type=jnp.float32).astype(
        jnp.bfloat16
    )
    send_g = (
        jnp.einsum("ts,td->sd", table_low, quantized, preferred_element_type=jnp.float32)
        * (send_prob * send_scale)[:, None]
    ).astype(jnp.bfloat16)
    bucket_shape = (ep_size, capacity, model_width)

    def exchange(a):
        return lax.all_to_all(a, "ep", split_axis=0, concat_axis=0, tiled=True)

    slot_x = exchange(send_x.reshape(bucket_shape)).reshape(slot_rows, model_width)
    all_x = lax.all_gather(slot_x, "dp", axis=0, tiled=True)
    slot_g = exchange(send_g.reshape(bucket_shape)).reshape(slot_rows, model_width)
    all_g = lax.all_gather(slot_g, "dp", axis=0, tiled=True)
    w_gate = gate_weight[0]
    w_up = up_weight[0]
    w_down = down_weight[0]
    activated, act_delta, gate_delta, up_delta = deltas(slot_x, slot_g, w_gate, w_up, w_down)
    slot_in = (
        jnp.dot(gate_delta, w_gate, preferred_element_type=jnp.float32)
        + jnp.dot(up_delta, w_up, preferred_element_type=jnp.float32)
    ).astype(jnp.bfloat16)
    slot_out = jnp.sum(activated * act_delta, axis=1)
    back_in = exchange(slot_in.reshape(bucket_shape))
    back_prob = exchange(slot_out.reshape(ep_size, capacity).astype(jnp.bfloat16))
    prob_grad = jnp.einsum("tks,s->tk", placement, back_prob.reshape(slot_rows)) / probs
    input_grad = jnp.einsum(
        "ts,sd->td",
        table_low,
        back_in.reshape(slot_rows, model_width),
        preferred_element_type=jnp.float32,
    ).astype(jnp.bfloat16)
    share = w_gate.shape[0] // dp_size
    first = lax.axis_index("dp") * share

    def mine(w):
        return lax.dynamic_slice_in_dim(w, first, share, 0)

    act_mine, _, gd_mine, ud_mine = deltas(all_x, all_g, mine(w_gate), mine(w_up), mine(w_down))
    gate_share = contract_first(gd_mine, all_x).astype(jnp.bfloat16)
    up_share = contract_first(ud_mine, all_x).astype(jnp.bfloat16)
    down_share = contract_first(act_mine.astype(jnp.bfloat16), all_g).astype(jnp.bfloat16)
    return (input_grad, prob_grad, gate_share[None], up_share[None], down_share[None])


def solution(mesh):
    return jax.shard_map(
        on_device,
        mesh=mesh,
        in_specs=(
            P(("ep", "dp"), None),
            P(("ep", "dp"), None),
            P(("ep", "dp"), None),
            P(("ep", "dp"), None),
            P(("ep", "dp"), None),
            P(),
            P("ep", None, None),
            P("ep", None, None),
            P("ep", None, None),
        ),
        out_specs=(
            P(("ep", "dp"), None),
            P(("ep", "dp"), None),
            P("ep", "dp", None),
            P("ep", "dp", None),
            P("ep", "dp", None),
        ),
        check_vma=False,
    )
```

profile of v0, /device:TPU:1, one launch (start us, length us, event | category | flops | bytes accessed | tf_op | source)
XLA Modules:
  0.0 248.0 jit_solution(7221112332950681031)
XLA Ops:
  13.6 1.9 convolution_convert_fusion
  15.6 2.5 reshape.94
  18.0 40.7 %all_to_all.24 = bf16[32,20,1536]{2,1,0:T(8,128)(2,1)} all-to-all(bf16[32,20,1536]{2,1,0:T(8,128)(2,1)S(1)} %reshape.94), channel_id=1, replica_groups=mesh['ep'=32,'dp'=4] {'ep'}, dimensions={0} | all-to-all | bytes 3932160 | tf_op jit(solution)/shard_map/all_to_all | solution.py:78
  58.7 4.1 %reshape.95 = bf16[640,1536]{1,0:T(8,128)(2,1)} reshape(bf16[32,20,1536]{2,1,0:T(8,128)(2,1)} %all_to_all.24) | data formatting | bytes 3932160 | tf_op jit(solution)/shard_map/reshape | solution.py:80
  63.1 2.1 multiply_convert_fusion.5
  65.2 2.5 reshape.92
  67.6 35.0 %all_to_all.25 = bf16[32,20,1536]{2,1,0:T(8,128)(2,1)} all-to-all(bf16[32,20,1536]{2,1,0:T(8,128)(2,1)S(1)} %reshape.92), channel_id=1, replica_groups=mesh['ep'=32,'dp'=4] {'ep'}, dimensions={0} | all-to-all | bytes 3932160 | tf_op jit(solution)/shard_map/all_to_all | solution.py:78
  102.6 4.1 %reshape.93 = bf16[640,1536]{1,0:T(8,128)(2,1)} reshape(bf16[32,20,1536]{2,1,0:T(8,128)(2,1)} %all_to_all.25) | data formatting | bytes 3932160 | tf_op jit(solution)/shard_map/reshape | solution.py:82
  106.8 5.3 %fusion.6 = f32[640,1536]{1,0:T(8,128)S(1)} fusion(bf16[640,1536]{1,0:T(8,128)(2,1)S(1)} %copy-done.2, bf16[1,1536,1536]{2,1,0:T(8,128)(2,1)} %param.16), kind=kOutput, calls=%fused_computation.6 | convolution fusion | flops 3019898880 | bytes 10616832 | tf_op jit(solution)/shard_map/dot_general | solution.py:10
  112.1 6.6 %fusion.2 = f32[640,1536]{1,0:T(8,128)S(1)} fusion(bf16[640,1536]{1,0:T(8,128)(2,1)S(1)} %copy-done.2, bf16[1,1536,1536]{2,1,0:T(8,128)(2,1)} %param.15), kind=kOutput, calls=%fused_computation.2 | convolution fusion | flops 3019898880 | bytes 10616832 | tf_op jit(solution)/shard_map/dot_general | solution.py:10
  118.8 5.4 %multiply_reduce_fusion = (bf16[640]{0:T(1024)(128)(2,1)S(1)}, f32[640,1536]{1,0:T(8,128)}) fusion(f32[640,1536]{1,0:T(8,128)S(1)} %fusion.6, f32[640,1536]{1,0:T(8,128)S(1)} %fusion.2, bf16[640,1536]{1,0:T(8,128)(2,1)S(1)} %copy-done.3, bf16[1,1536,1536]{2,1,0:T(8,128)(2,1)S(1)} %bitcast.64), kind=kOutput, calls=%fused_computation.15 | convolution fusion | flops 3028745728 | bytes 18482432 | tf_op jit(solution)/shard_map/dot_general | solution.py:10
  124.9 3.8 %all-to-all-start.3 = ((bf16[32,1,20]{2,1,0:T(2,128)(2,1)}), bf16[32,1,20]{2,1,0:T(2,128)(2,1)S(1)}, u32[]{:S(2)}, u32[]{:S(2)}) async-start(bf16[32,1,20]{2,1,0:T(2,128)(2,1)} %convert_element_type.97), calls=%async_computation.3 | async-start | bytes 32768 | tf_op jit(solution)/shard_map/all_to_all | solution.py:78
  128.8 8.9 %fusion = f32[640,1536]{1,0:T(8,128)S(1)} fusion(bf16[1,1536,1536]{2,1,0:T(8,128)(2,1)} %param.15, f32[640,1536]{1,0:T(8,128)} %get-tuple-element.12, f32[640,1536]{1,0:T(8,128)} %copy-done.9, f32[640,1536]{1,0:T(8,128)} %copy-done.11), kind=kOutput, calls=%fused_computation | convolution fusion | flops 3031695360 | bytes 20447232 | tf_op jit(solution)/shard_map/dot_general | solution.py:89
  137.7 5.8 %add_convert_fusion = bf16[640,1536]{1,0:T(8,128)(2,1)S(1)} fusion(f32[640,1536]{1,0:T(8,128)S(1)} %fusion, bf16[1,1536,1536]{2,1,0:T(8,128)(2,1)} %param.16, f32[640,1536]{1,0:T(8,128)S(1)} %copy-done.13, f32[640,1536]{1,0:T(8,128)S(1)} %copy-done.10), kind=kOutput, calls=%fused_computation.16 | convolution fusion | flops 3028746240 | bytes 18481152 | tf_op jit(solution)/shard_map/dot_general | solution.py:90
  143.6 2.1 reshape.96
  145.7 7.3 %all-to-all-start.2 = ((bf16[32,20,1536]{2,1,0:T(8,128)(2,1)}), bf16[32,20,1536]{2,1,0:T(8,128)(2,1)S(1)}, u32[]{:S(2)}, u32[]{:S(2)}) async-start(bf16[32,20,1536]{2,1,0:T(8,128)(2,1)} %reshape.96), calls=%async_computation.2 | async-start | bytes 4718592 | tf_op jit(solution)/shard_map/all_to_all | solution.py:78
  154.0 30.6 %all-to-all-done.2 = bf16[32,20,1536]{2,1,0:T(8,128)(2,1)S(1)} async-done(((bf16[32,20,1536]{2,1,0:T(8,128)(2,1)}), bf16[32,20,1536]{2,1,0:T(8,128)(2,1)S(1)}, u32[]{:S(2)}, u32[]{:S(2)}) %all-to-all-start.2) | async-done | bytes 1966112 | tf_op jit(solution)/shard_map/all_to_all | solution.py:78
  186.1 9.9 %fusion.25 = f32[2560,384]{1,0:T(8,128)} fusion(bf16[2560,1536]{1,0:T(8,128)(2,1)} %all-gather.5.cloned.1.call-done, bf16[1,1536,1536]{2,1,0:T(8,128)(2,1)} %param.15, s32[]{:T(128)S(6)} %select_n.2), kind=kOutput, calls=%fused_computation.41 | convolution fusion | flops 3019898880 | bytes 12976132 | tf_op jit(solution)/shard_map/dot_general | solution.py:10
  196.0 7.5 %convolution_add_fusion = f32[2560,384]{1,0:T(8,128)} fusion(bf16[2560,1536]{1,0:T(8,128)(2,1)S(1)} %copy-done.6, bf16[1,1536,1536]{2,1,0:T(8,128)(2,1)} %param.16, s32[]{:T(128)S(6)} %select_n.2), kind=kOutput, calls=%fused_computation.10 | convolution fusion | flops 3020881920 | bytes 12976132 | tf_op jit(solution)/shard_map/dot_general | solution.py:10
  203.4 16.9 %all-gather.3.cloned.1.call-done = bf16[2560,1536]{1,0:T(8,128)(2,1)} async-done(((bf16[640,1536]{1,0:T(8,128)(2,1)}), bf16[2560,1536]{1,0:T(8,128)(2,1)}) %all-gather.3.cloned.1.call-update) | async-done | bytes 7864336 | tf_op jit(solution)/shard_map/all_gather | solution.py:83
  220.3 7.4 %fusion.28 = f32[2560,384]{1,0:T(8,128)S(1)} fusion(bf16[2560,1536]{1,0:T(8,128)(2,1)} %all-gather.3.cloned.1.call-done, bf16[1,1536,1536]{2,1,0:T(8,128)(2,1)} %param.17, s32[]{:T(128)S(6)} %select_n.2), kind=kOutput, calls=%fused_computation.44 | convolution fusion | flops 3019898880 | bytes 12976132 | tf_op jit(solution)/shard_map/dot_general | solution.py:10
  227.7 4.4 %fusion.15 = bf16[1,384,1536]{2,1,0:T(8,128)(2,1)} fusion(bf16[2560,1536]{1,0:T(8,128)(2,1)S(1)} %copy-done.7, f32[2560,384]{1,0:T(8,128)S(1)} %fusion.28, f32[2560,384]{1,0:T(8,128)S(1)} %copy-done.8), kind=kOutput, calls=%fused_computation.28 | convolution fusion | flops 3027369984 | bytes 16908288 | tf_op jit(solution)/shard_map/dot_general | solution.py:16
  232.2 4.5 %fusion.14 = bf16[1,384,1536]{2,1,0:T(8,128)(2,1)} fusion(bf16[2560,1536]{1,0:T(8,128)(2,1)S(1)} %copy-done.7, f32[2560,384]{1,0:T(8,128)S(1)} %fusion.28, f32[2560,384]{1,0:T(8,128)S(1)} %copy-done.12, f32[2560,384]{1,0:T(8,128)S(1)} %copy-done.8), kind=kOutput, calls=%fused_computation.27 | convolution fusion | flops 3031302144 | bytes 20840448 | tf_op jit(solution)/shard_map/dot_general | solution.py:16
  236.7 4.4 %fusion.16 = bf16[1,384,1536]{2,1,0:T(8,128)(2,1)} fusion(bf16[2560,1536]{1,0:T(8,128)(2,1)S(1)} %bitcast.62, f32[2560,384]{1,0:T(8,128)S(1)} %copy-done.12, f32[2560,384]{1,0:T(8,128)S(1)} %copy-done.8), kind=kOutput, calls=%fused_computation.29 | convolution fusion | flops 3027369984 | bytes 16908288 | tf_op jit(solution)/shard_map/dot_general | solution.py:16
  (65 shorter events, 9.9 us)
Async XLA Ops:
  7.2 6.5 %copy-start = (bf16[128,1536]{1,0:T(8,128)(2,1)S(1)}, bf16[128,1536]{1,0:T(8,128)(2,1)}, u32[]{:S(2)}) copy-start(bf16[128,1536]{1,0:T(8,128)(2,1)} %param.10) | copy-start | bytes 1179652
  7.2 178.9 %all-gather.5.cloned.1.call-start = ((), (), s32[]{:S(2)}) async-start(), calls=%async_computation.5 | async-start | bytes 9830400 | tf_op jit(solution)/shard_map/all_gather | solution.py:81
  58.7 4.3 %copy-start.4 = (f32[128,1536]{1,0:T(8,128)S(1)}, f32[128,1536]{1,0:T(8,128)}, u32[]{:S(2)}) copy-start(f32[128,1536]{1,0:T(8,128)} %param.9) | copy-start | bytes 2359300
  62.8 157.5 %all-gather.3.cloned.1.call-start = ((), (), s32[]{:S(2)}) async-start(), calls=%async_computation.4 | async-start | bytes 9830400 | tf_op jit(solution)/shard_map/all_gather | solution.py:83
  102.6 4.2 %copy-start.2 = (bf16[640,1536]{1,0:T(8,128)(2,1)S(1)}, bf16[640,1536]{1,0:T(8,128)(2,1)}, u32[]{:S(2)}) copy-start(bf16[640,1536]{1,0:T(8,128)(2,1)} %reshape.95) | copy-start | bytes 5898244
  106.8 12.0 %slice-start.2 = ((s8[4718592]{0:T(1024)(128)(4,1)}), s8[4194304]{0:T(1024)(128)(4,1)S(1)}, s32[]{:S(2)}) async-start(s8[4718592]{0:T(1024)(128)(4,1)} %bitcast.63), calls=%async_computation.8 | async-start | bytes 8388608
  112.1 6.7 %copy-start.11 = (f32[640,1536]{1,0:T(8,128)}, f32[640,1536]{1,0:T(8,128)S(1)}, u32[]{:S(2)}) copy-start(f32[640,1536]{1,0:T(8,128)S(1)} %fusion.6) | copy-start | bytes 11796484
  112.1 6.7 %copy-start.3 = (bf16[640,1536]{1,0:T(8,128)(2,1)S(1)}, bf16[640,1536]{1,0:T(8,128)(2,1)}, u32[]{:S(2)}) copy-start(bf16[640,1536]{1,0:T(8,128)(2,1)} %reshape.93) | copy-start | bytes 5898244
  112.1 6.7 %slice-start.3 = ((s8[4718592]{0:T(1024)(128)(4,1)}), s8[524288]{0:T(1024)(128)(4,1)S(1)}, s32[]{:S(2)}) async-start(s8[4718592]{0:T(1024)(128)(4,1)} %bitcast.63), calls=%async_computation.9 | async-start | bytes 1048576
  118.8 5.4 %copy-start.9 = (f32[640,1536]{1,0:T(8,128)}, f32[640,1536]{1,0:T(8,128)S(1)}, u32[]{:S(2)}) copy-start(f32[640,1536]{1,0:T(8,128)S(1)} %fusion.2) | copy-start | bytes 11796484
  124.9 20.7 %all-to-all-start.3 = ((bf16[32,1,20]{2,1,0:T(2,128)(2,1)}), bf16[32,1,20]{2,1,0:T(2,128)(2,1)S(1)}, u32[]{:S(2)}, u32[]{:S(2)}) async-start(bf16[32,1,20]{2,1,0:T(2,128)(2,1)} %convert_element_type.97), calls=%async_computation.3 | async-start | bytes 32768 | tf_op jit(solution)/shard_map/all_to_all | solution.py:78
  128.8 9.0 %copy-start.10 = (f32[640,1536]{1,0:T(8,128)S(1)}, f32[640,1536]{1,0:T(8,128)}, u32[]{:S(2)}) copy-start(f32[640,1536]{1,0:T(8,128)} %copy-done.9) | copy-start | bytes 11796484
  128.8 9.0 %copy-start.13 = (f32[640,1536]{1,0:T(8,128)S(1)}, f32[640,1536]{1,0:T(8,128)}, u32[]{:S(2)}) copy-start(f32[640,1536]{1,0:T(8,128)} %get-tuple-element.12) | copy-start | bytes 11796484
  143.6 9.8 %copy-start.5 = (f32[128,4]{0,1:T(4,128)S(1)}, f32[128,4]{0,1:T(4,128)}, u32[]{:S(2)}) copy-start(f32[128,4]{0,1:T(4,128)} %param.11) | copy-start | bytes 6148
  145.7 38.9 %all-to-all-start.2 = ((bf16[32,20,1536]{2,1,0:T(8,128)(2,1)}), bf16[32,20,1536]{2,1,0:T(8,128)(2,1)S(1)}, u32[]{:S(2)}, u32[]{:S(2)}) async-start(bf16[32,20,1536]{2,1,0:T(8,128)(2,1)} %reshape.96), calls=%async_computation.2 | async-start | bytes 4718592 | tf_op jit(solution)/shard_map/all_to_all | solution.py:78
  186.1 9.9 %copy-start.6 = (bf16[2560,1536]{1,0:T(8,128)(2,1)S(1)}, bf16[2560,1536]{1,0:T(8,128)(2,1)}, u32[]{:S(2)}) copy-start(bf16[2560,1536]{1,0:T(8,128)(2,1)} %all-gather.5.cloned.1.call-done) | copy-start | bytes 23592964
  220.3 7.4 %copy-start.7 = (bf16[2560,1536]{1,0:T(8,128)(2,1)S(1)}, bf16[2560,1536]{1,0:T(8,128)(2,1)}, u32[]{:S(2)}) copy-start(bf16[2560,1536]{1,0:T(8,128)(2,1)} %all-gather.5.cloned.1.call-done) | copy-start | bytes 23592964
  220.3 7.4 %copy-start.8 = (f32[2560,384]{1,0:T(8,128)S(1)}, f32[2560,384]{1,0:T(8,128)}, u32[]{:S(2)}) copy-start(f32[2560,384]{1,0:T(8,128)} %fusion.25) | copy-start | bytes 11796484
  227.7 4.5 %copy-start.12 = (f32[2560,384]{1,0:T(8,128)S(1)}, f32[2560,384]{1,0:T(8,128)}, u32[]{:S(2)}) copy-start(f32[2560,384]{1,0:T(8,128)} %convolution_add_fusion) | copy-start | bytes 11796484
  227.7 9.0 %slice-start = ((s8[7864320]{0:T(1024)(128)(4,1)}), s8[4194304]{0:T(1024)(128)(4,1)S(1)}, s32[]{:S(2)}) async-start(s8[7864320]{0:T(1024)(128)(4,1)} %bitcast.61), calls=%async_computation.6 | async-start | bytes 8388608
  232.2 4.6 %slice-start.1 = ((s8[7864320]{0:T(1024)(128)(4,1)}), s8[3670016]{0:T(1024)(128)(4,1)S(1)}, s32[]{:S(2)}) async-start(s8[7864320]{0:T(1024)(128)(4,1)} %bitcast.61), calls=%async_computation.7 | async-start | bytes 7340032
  236.7 4.4 %copy-start.1 = (bf16[128,1536]{1,0:T(8,128)(2,1)S(1)}, bf16[128,1536]{1,0:T(8,128)(2,1)}, u32[]{:S(2)}) copy-start(bf16[128,1536]{1,0:T(8,128)(2,1)} %param.10) | copy-start | bytes 1179652
Sparse Core Ops, SparseCore 0:
  62.9 76.0 all-gather.4
  140.7 79.5 all-gather.2
where the time goes:
time: 249 us; the launch traced here: 248 us
  matrix products  76.9 us (31%)
  blocking collectives  75.7 us (30%)
  waiting for transfers between devices  47.5 us (19%)
  local copies, waits for them, and re-layouts  16.4 us (7%)
  between operations  14.4 us (6%)
  starting transfers between devices  11.2 us (4%)
  other arithmetic  5.9 us (2%)
    all_to_all x2, blocking collectives, exchange(): return lax.all_to_all(a, 'ep', split_axis=0, concat_axis=0, tiled=True)  75.7 us
    dot_general x6, matrix products, contract_last(): lax.dot_general(first_op, second_op, (((1,), (1,)), ((), ())), preferred_...  42 us
    all_to_all x2, waiting for transfers between devices, exchange(): return lax.all_to_all(a, 'ep', split_axis=0, concat_axis=0, tiled=True)  30.6 us
    all_gather x1, waiting for transfers between devices, on_device(): all_g = lax.all_gather(slot_g, 'dp', axis=0, tiled=True)  16.9 us
    dot_general x3, matrix products, contract_first(): lax.dot_general(first_op, second_op, (((0,), (0,)), ((), ())), preferred_...  13.4 us
    all_to_all x2, starting transfers between devices, exchange(): return lax.all_to_all(a, 'ep', split_axis=0, concat_axis=0, tiled=True)  11.1 us
    dot_general x1, matrix products, on_device(): jnp.dot(gate_delta, w_gate, preferred_element_type=jnp.float32)  8.95 us
    dot_general x1, matrix products, on_device(): jnp.dot(up_delta, w_up, preferred_element_type=jnp.float32)  5.8 us
  transfers between devices with their start and end apart: 4, of which 2 were waited for; matrix products, arithmetic and copies ran while one was open for 26% of the time, Pallas kernels for 0%

commit v1 on v0

--- a/solution.py
+++ b/solution.py
@@ -4,6 +4,27 @@
 from jax.sharding import PartitionSpec as P
 
 sharpness = 1.702
+
+
+def collect(x, axis, dim):
+    count, index, width = (lax.axis_size(axis), lax.axis_index(axis), x.shape[dim])
+    ahead = [(i, (i + 1) % count) for i in range(count)]
+    downward = [(i, (i - 1) % count) for i in range(count)]
+    out = jnp.zeros((*x.shape[:dim], count * width, *x.shape[dim + 1 :]), x.dtype)
+    out = lax.dynamic_update_slice_in_dim(out, x, index * width, axis=dim)
+    from_left = from_right = x
+    middle = count // 2
+    for hop in range(1, middle + 1):
+        from_left = lax.ppermute(from_left, axis, ahead)
+        out = lax.dynamic_update_slice_in_dim(
+            out, from_left, (index - hop) % count * width, axis=dim
+        )
+        if hop < count - middle:
+            from_right = lax.ppermute(from_right, axis, downward)
+            out = lax.dynamic_update_slice_in_dim(
+                out, from_right, (index + hop) % count * width, axis=dim
+            )
+    return out
 
 
 def contract_last(first_op, second_op):
@@ -80,7 +101,7 @@
     slot_x = exchange(send_x.reshape(bucket_shape)).reshape(slot_rows, model_width)
     all_x = lax.all_gather(slot_x, "dp", axis=0, tiled=True)
     slot_g = exchange(send_g.reshape(bucket_shape)).reshape(slot_rows, model_width)
-    all_g = lax.all_gather(slot_g, "dp", axis=0, tiled=True)
+    all_g = collect(slot_g, "dp", 0)
     w_gate = gate_weight[0]
     w_up = up_weight[0]
     w_down = down_weight[0]

time: 249 us -> 275 us (1.10)
  waiting for transfers between devices: 47.5 us -> 87 us
  blocking collectives: 75.7 us -> 36.7 us
  starting transfers between devices: 11.2 us -> 23.6 us
  local copies, waits for them, and re-layouts: 16.4 us -> 27.8 us
    ppermute x0 -> x3, waiting for transfers between devices: none -> 55.2 us  [the longest x2 46.7 us: collect(): from_left = lax.ppermute(from_left, axis, ahead)]
    all_to_all x2 -> x1, blocking collectives: 75.7 us -> 36.7 us  [exchange(): return lax.all_to_all(a, 'ep', split_axis=0, concat_axis=0, tiled=True)]
    all_gather x1 -> x0, waiting for transfers between devices: 16.9 us -> none  [on_device(): all_g = lax.all_gather(slot_g, 'dp', axis=0, tiled=True)]
    dynamic_update_slice x0 -> x4, local copies, waits for them, and re-layouts: none -> 10.3 us  [the longest x2 5.95 us: collect(): lax.dynamic_update_slice_in_dim(out, from_left, (index - hop) % count * w...]
    all_to_all x2 -> x3, starting transfers between devices: 11.1 us -> 20.9 us  [exchange(): return lax.all_to_all(a, 'ep', split_axis=0, concat_axis=0, tiled=True)]
    broadcast_in_dim x0 -> x1, local copies, waits for them, and re-layouts: none -> 3.58 us  [collect(): jnp.zeros((*x.shape[:dim], count * width, *x.shape[dim + 1:]), x.dtype)]
    dot_general x3, matrix products: 13.4 us -> 16.9 us  [contract_first(): lax.dot_general(first_op, second_op, (((0,), (0,)), ((), ())), preferred_...]
    all_to_all x2 -> x3, waiting for transfers between devices: 30.6 us -> 31.7 us  [exchange(): return lax.all_to_all(a, 'ep', split_axis=0, concat_axis=0, tiled=True)]
  transfers between devices with their start and end apart: 4 -> 7, of which waited for: 2 -> 5; matrix products, arithmetic and copies ran while one was open for 26% -> 26% of each run, Pallas kernels for 0% -> 0%
where the time goes in v1:
time: 275 us; the launch traced here: 274 us
  waiting for transfers between devices  87 us (32%)
  matrix products  78.5 us (29%)
  blocking collectives  36.7 us (13%)
  local copies, waits for them, and re-layouts  27.8 us (10%)
  starting transfers between devices  23.6 us (9%)
  between operations  14.3 us (5%)
  other arithmetic  5.91 us (2%)
    ppermute x2, waiting for transfers between devices, collect(): from_left = lax.ppermute(from_left, axis, ahead)  46.7 us
    dot_general x6, matrix products, contract_last(): lax.dot_general(first_op, second_op, (((1,), (1,)), ((), ())), preferred_...  40.3 us
    all_to_all x1, blocking collectives, exchange(): return lax.all_to_all(a, 'ep', split_axis=0, concat_axis=0, tiled=True)  36.7 us
    all_to_all x3, waiting for transfers between devices, exchange(): return lax.all_to_all(a, 'ep', split_axis=0, concat_axis=0, tiled=True)  31.7 us
    all_to_all x3, starting transfers between devices, exchange(): return lax.all_to_all(a, 'ep', split_axis=0, concat_axis=0, tiled=True)  20.9 us
    dot_general x3, matrix products, contract_first(): lax.dot_general(first_op, second_op, (((0,), (0,)), ((), ())), preferred_...  16.9 us
    dot_general x1, matrix products, on_device(): jnp.dot(gate_delta, w_gate, preferred_element_type=jnp.float32)  8.94 us
    ppermute x1, waiting for transfers between devices, collect(): from_right = lax.ppermute(from_right, axis, downward)  8.51 us
  transfers between devices with their start and end apart: 7, of which 5 were waited for; matrix products, arithmetic and copies ran while one was open for 26% of the time, Pallas kernels for 0%

profile of v1, /device:TPU:1, one launch (start us, length us, event | category | flops | bytes accessed | tf_op | source)
XLA Modules:
  0.0 273.9 jit_solution(18420180064385169163)
XLA Ops:
  16.3 9.4 %all-to-all-start.1 = ((bf16[32,20,1536]{2,1,0:T(8,128)(2,1)}), bf16[32,20,1536]{2,1,0:T(8,128)(2,1)S(1)}, u32[]{:S(2)}, u32[]{:S(2)}) async-start(bf16[32,20,1536]{2,1,0:T(8,128)(2,1)} %reshape.94), calls=%async_computation.1 | async-start | bytes 4718592 | tf_op jit(solution)/shard_map/all_to_all | solution.py:99
  26.0 31.3 %all-to-all-done.1 = bf16[32,20,1536]{2,1,0:T(8,128)(2,1)S(1)} async-done(((bf16[32,20,1536]{2,1,0:T(8,128)(2,1)}), bf16[32,20,1536]{2,1,0:T(8,128)(2,1)S(1)}, u32[]{:S(2)}, u32[]{:S(2)}) %all-to-all-start.1) | async-done | bytes 1966112 | tf_op jit(solution)/shard_map/all_to_all | solution.py:99
  59.4 3.1 %multiply_convert_fusion.5 = bf16[640,1536]{1,0:T(8,128)(2,1)} fusion(bf16[128,640]{0,1:T(8,128)(2,1)S(1)} %convert_element_type.81, f32[640]{0:T(1024)S(1)} %mul.148, f32[128,1536]{1,0:T(8,128)} %param.9, f32[128]{0:T(128)S(1)} %broadcast_maximum_fusion), kind=kOutput, calls=%fused_computation.20 | convolution fusion | flops 254017536 | bytes 2919424 | tf_op jit(solution)/shard_map/ts,td->sd/dot_general | solution.py:93
  65.0 36.7 %all_to_all.24 = bf16[32,20,1536]{2,1,0:T(8,128)(2,1)} all-to-all(bf16[32,20,1536]{2,1,0:T(8,128)(2,1)S(1)} %reshape.92), channel_id=1, replica_groups=mesh['ep'=32,'dp'=4] {'ep'}, dimensions={0} | all-to-all | bytes 3932160 | tf_op jit(solution)/shard_map/all_to_all | solution.py:99
  101.7 4.1 %reshape.93 = bf16[640,1536]{1,0:T(8,128)(2,1)} reshape(bf16[32,20,1536]{2,1,0:T(8,128)(2,1)} %all_to_all.24) | data formatting | bytes 3932160 | tf_op jit(solution)/shard_map/reshape | solution.py:103
  107.0 5.3 %fusion.6 = f32[640,1536]{1,0:T(8,128)S(1)} fusion(bf16[640,1536]{1,0:T(8,128)(2,1)S(1)} %copy-done.2, bf16[1,1536,1536]{2,1,0:T(8,128)(2,1)} %param.16), kind=kOutput, calls=%fused_computation.6 | convolution fusion | flops 3019898880 | bytes 10616832 | tf_op jit(solution)/shard_map/dot_general | solution.py:31
  112.4 6.6 %fusion.2 = f32[640,1536]{1,0:T(8,128)S(1)} fusion(bf16[640,1536]{1,0:T(8,128)(2,1)S(1)} %copy-done.2, bf16[1,1536,1536]{2,1,0:T(8,128)(2,1)} %param.15), kind=kOutput, calls=%fused_computation.2 | convolution fusion | flops 3019898880 | bytes 10616832 | tf_op jit(solution)/shard_map/dot_general | solution.py:31
  119.0 5.3 %multiply_reduce_fusion = (bf16[640]{0:T(1024)(128)(2,1)S(1)}, f32[640,1536]{1,0:T(8,128)}) fusion(f32[640,1536]{1,0:T(8,128)S(1)} %fusion.6, f32[640,1536]{1,0:T(8,128)S(1)} %fusion.2, bf16[640,1536]{1,0:T(8,128)(2,1)S(1)} %copy-done.3, bf16[1,1536,1536]{2,1,0:T(8,128)(2,1)S(1)} %bitcast.62), kind=kOutput, calls=%fused_computation.15 | convolution fusion | flops 3028745728 | bytes 18482432 | tf_op jit(solution)/shard_map/dot_general | solution.py:31
  125.1 4.0 %all-to-all-start.3 = ((bf16[32,1,20]{2,1,0:T(2,128)(2,1)}), bf16[32,1,20]{2,1,0:T(2,128)(2,1)S(1)}, u32[]{:S(2)}, u32[]{:S(2)}) async-start(bf16[32,1,20]{2,1,0:T(2,128)(2,1)} %convert_element_type.97), calls=%async_computation.3 | async-start | bytes 32768 | tf_op jit(solution)/shard_map/all_to_all | solution.py:99
  129.2 8.9 %fusion = f32[640,1536]{1,0:T(8,128)S(1)} fusion(bf16[1,1536,1536]{2,1,0:T(8,128)(2,1)} %param.15, f32[640,1536]{1,0:T(8,128)} %get-tuple-element.12, f32[640,1536]{1,0:T(8,128)} %copy-done.8, f32[640,1536]{1,0:T(8,128)} %copy-done.10), kind=kOutput, calls=%fused_computation | convolution fusion | flops 3031695360 | bytes 20447232 | tf_op jit(solution)/shard_map/dot_general | solution.py:110
  138.1 5.8 %add_convert_fusion = bf16[640,1536]{1,0:T(8,128)(2,1)S(1)} fusion(f32[640,1536]{1,0:T(8,128)S(1)} %fusion, bf16[1,1536,1536]{2,1,0:T(8,128)(2,1)} %param.16, f32[640,1536]{1,0:T(8,128)S(1)} %copy-done.11, f32[640,1536]{1,0:T(8,128)S(1)} %copy-done.9), kind=kOutput, calls=%fused_computation.16 | convolution fusion | flops 3028746240 | bytes 18481152 | tf_op jit(solution)/shard_map/dot_general | solution.py:111
  146.1 7.4 %all-to-all-start.2 = ((bf16[32,20,1536]{2,1,0:T(8,128)(2,1)}), bf16[32,20,1536]{2,1,0:T(8,128)(2,1)S(1)}, u32[]{:S(2)}, u32[]{:S(2)}) async-start(bf16[32,20,1536]{2,1,0:T(8,128)(2,1)} %reshape.96), calls=%async_computation.2 | async-start | bytes 4718592 | tf_op jit(solution)/shard_map/all_to_all | solution.py:99
  154.9 23.7 %collective-permute-done = bf16[640,1536]{1,0:T(8,128)(2,1)} collective-permute-done((bf16[640,1536]{1,0:T(8,128)(2,1)}, bf16[640,1536]{1,0:T(8,128)(2,1)}, u32[]{:S(2)}, u32[]{:S(2)}) %collective-permute-start) | collective-permute-done | bytes 1966112 | tf_op jit(solution)/shard_map/ppermute | solution.py:18
  178.6 3.6 %broadcast_in_dim.8 = bf16[2560,1536]{1,0:T(8,128)(2,1)} broadcast(bf16[]{:T(256)} %constant.47.clone.1), dimensions={} | broadcast | bytes 7864322 | tf_op jit(solution)/shard_map/broadcast_in_dim | solution.py:13
  186.5 3.0 %constant_dynamic-update-slice_fusion.2 = bf16[2560,1536]{1,0:T(8,128)(2,1)} fusion(bf16[2560,1536]{1,0:T(8,128)(2,1)} %constant_dynamic-update-slice_fusion.3, bf16[640,1536]{1,0:T(8,128)(2,1)} %collective-permute-done, s32[]{:T(128)S(6)} %select_n.34), kind=kLoop, calls=%fused_computation.73 | loop fusion | bytes 3932164 | tf_op jit(solution)/shard_map/dynamic_update_slice | solution.py:19
  189.5 8.5 %collective-permute-done.1 = bf16[640,1536]{1,0:T(8,128)(2,1)} collective-permute-done((bf16[640,1536]{1,0:T(8,128)(2,1)}, bf16[640,1536]{1,0:T(8,128)(2,1)}, u32[]{:S(2)}, u32[]{:S(2)}) %collective-permute-start.1) | collective-permute-done | bytes 1966112 | tf_op jit(solution)/shard_map/ppermute | solution.py:23
  200.9 23.0 %collective-permute-done.2 = bf16[640,1536]{1,0:T(8,128)(2,1)} collective-permute-done((bf16[640,1536]{1,0:T(8,128)(2,1)}, bf16[640,1536]{1,0:T(8,128)(2,1)}, u32[]{:S(2)}, u32[]{:S(2)}) %collective-permute-start.2) | collective-permute-done | bytes 1966112 | tf_op jit(solution)/shard_map/ppermute | solution.py:18
  224.0 3.0 %constant_dynamic-update-slice_fusion = bf16[2560,1536]{1,0:T(8,128)(2,1)} fusion(bf16[2560,1536]{1,0:T(8,128)(2,1)} %constant_dynamic-update-slice_fusion.1, bf16[640,1536]{1,0:T(8,128)(2,1)} %collective-permute-done.2, s32[]{:T(128)S(6)} %select_n.38), kind=kLoop, calls=%fused_computation.71 | loop fusion | bytes 3932164 | tf_op jit(solution)/shard_map/dynamic_update_slice | solution.py:19
  227.0 9.8 %fusion.28 = f32[2560,384]{1,0:T(8,128)} fusion(bf16[2560,1536]{1,0:T(8,128)(2,1)} %constant_dynamic-update-slice_fusion, bf16[1,1536,1536]{2,1,0:T(8,128)(2,1)} %param.17, s32[]{:T(128)S(6)} %select_n.39), kind=kOutput, calls=%fused_computation.44 | convolution fusion | flops 3019898880 | bytes 12976132 | tf_op jit(solution)/shard_map/dot_general | solution.py:31
  236.8 7.7 %convolution_add_fusion = f32[2560,384]{1,0:T(8,128)S(1)} fusion(bf16[2560,1536]{1,0:T(8,128)(2,1)} %all-gather.2.cloned.1.call-done, bf16[1,1536,1536]{2,1,0:T(8,128)(2,1)} %param.16, s32[]{:T(128)S(6)} %select_n.39), kind=kOutput, calls=%fused_computation.10 | convolution fusion | flops 3020881920 | bytes 12976132 | tf_op jit(solution)/shard_map/dot_general | solution.py:31
  244.5 5.6 %fusion.25 = f32[2560,384]{1,0:T(8,128)S(1)} fusion(bf16[2560,1536]{1,0:T(8,128)(2,1)S(1)} %copy-done.6, bf16[1,1536,1536]{2,1,0:T(8,128)(2,1)} %param.15, s32[]{:T(128)S(6)} %select_n.39), kind=kOutput, calls=%fused_computation.41 | convolution fusion | flops 3019898880 | bytes 12976132 | tf_op jit(solution)/shard_map/dot_general | solution.py:31
  250.1 7.9 %fusion.16 = bf16[1,384,1536]{2,1,0:T(8,128)(2,1)} fusion(bf16[2560,1536]{1,0:T(8,128)(2,1)} %constant_dynamic-update-slice_fusion, f32[2560,384]{1,0:T(8,128)S(1)} %convolution_add_fusion, f32[2560,384]{1,0:T(8,128)S(1)} %fusion.25), kind=kOutput, calls=%fused_computation.29 | convolution fusion | flops 3027369984 | bytes 16908288 | tf_op jit(solution)/shard_map/dot_general | solution.py:37
  258.0 4.5 %fusion.14 = bf16[1,384,1536]{2,1,0:T(8,128)(2,1)} fusion(bf16[2560,1536]{1,0:T(8,128)(2,1)S(1)} %copy-done.6, f32[2560,384]{1,0:T(8,128)S(1)} %copy-done.7, f32[2560,384]{1,0:T(8,128)S(1)} %convolution_add_fusion, f32[2560,384]{1,0:T(8,128)S(1)} %fusion.25), kind=kOutput, calls=%fused_computation.27 | convolution fusion | flops 3031302144 | bytes 20840448 | tf_op jit(solution)/shard_map/dot_general | solution.py:37
  262.6 4.4 %fusion.15 = bf16[1,384,1536]{2,1,0:T(8,128)(2,1)} fusion(bf16[2560,1536]{1,0:T(8,128)(2,1)S(1)} %copy-done.6, f32[2560,384]{1,0:T(8,128)S(1)} %copy-done.7, f32[2560,384]{1,0:T(8,128)S(1)} %fusion.25), kind=kOutput, calls=%fused_computation.28 | convolution fusion | flops 3027369984 | bytes 16908288 | tf_op jit(solution)/shard_map/dot_general | solution.py:37
  (65 shorter events, 26.8 us)
Async XLA Ops:
  7.2 6.4 %copy-start = (bf16[128,1536]{1,0:T(8,128)(2,1)S(1)}, bf16[128,1536]{1,0:T(8,128)(2,1)}, u32[]{:S(2)}) copy-start(bf16[128,1536]{1,0:T(8,128)(2,1)} %param.10) | copy-start | bytes 1179652
  16.3 40.9 %all-to-all-start.1 = ((bf16[32,20,1536]{2,1,0:T(8,128)(2,1)}), bf16[32,20,1536]{2,1,0:T(8,128)(2,1)S(1)}, u32[]{:S(2)}, u32[]{:S(2)}) async-start(bf16[32,20,1536]{2,1,0:T(8,128)(2,1)} %reshape.94), calls=%async_computation.1 | async-start | bytes 4718592 | tf_op jit(solution)/shard_map/all_to_all | solution.py:99
  25.8 211.0 %all-gather.2.cloned.1.call-start = ((), (), s32[]{:S(2)}) async-start(), calls=%async_computation.4 | async-start | bytes 9830400 | tf_op jit(solution)/shard_map/all_gather | solution.py:102
  101.7 5.4 %copy-start.2 = (bf16[640,1536]{1,0:T(8,128)(2,1)S(1)}, bf16[640,1536]{1,0:T(8,128)(2,1)}, u32[]{:S(2)}) copy-start(bf16[640,1536]{1,0:T(8,128)(2,1)} %reshape.95) | copy-start | bytes 5898244
  105.7 72.8 %collective-permute-start = (bf16[640,1536]{1,0:T(8,128)(2,1)}, bf16[640,1536]{1,0:T(8,128)(2,1)}, u32[]{:S(2)}, u32[]{:S(2)}) collective-permute-start(bf16[640,1536]{1,0:T(8,128)(2,1)} %reshape.93), channel_id=1, source_target_pairs={{0,1},{1,2},{2,3},{3,0},{4,5},{5,6},{6,7},{7,4},{8,9},{9,10},{10,1... | collective-permute-start | bytes 5898248 | tf_op jit(solution)/shard_map/ppermute | solution.py:18
  107.0 11.9 %slice-start = ((s8[4718592]{0:T(1024)(128)(4,1)}), s8[4194304]{0:T(1024)(128)(4,1)S(1)}, s32[]{:S(2)}) async-start(s8[4718592]{0:T(1024)(128)(4,1)} %bitcast.61), calls=%async_computation.5 | async-start | bytes 8388608
  112.3 6.6 %copy-start.10 = (f32[640,1536]{1,0:T(8,128)}, f32[640,1536]{1,0:T(8,128)S(1)}, u32[]{:S(2)}) copy-start(f32[640,1536]{1,0:T(8,128)S(1)} %fusion.6) | copy-start | bytes 11796484
  112.4 6.6 %copy-start.3 = (bf16[640,1536]{1,0:T(8,128)(2,1)S(1)}, bf16[640,1536]{1,0:T(8,128)(2,1)}, u32[]{:S(2)}) copy-start(bf16[640,1536]{1,0:T(8,128)(2,1)} %reshape.93) | copy-start | bytes 5898244
  112.4 6.6 %slice-start.1 = ((s8[4718592]{0:T(1024)(128)(4,1)}), s8[524288]{0:T(1024)(128)(4,1)S(1)}, s32[]{:S(2)}) async-start(s8[4718592]{0:T(1024)(128)(4,1)} %bitcast.61), calls=%async_computation.6 | async-start | bytes 1048576
  119.0 5.4 %copy-start.8 = (f32[640,1536]{1,0:T(8,128)}, f32[640,1536]{1,0:T(8,128)S(1)}, u32[]{:S(2)}) copy-start(f32[640,1536]{1,0:T(8,128)S(1)} %fusion.2) | copy-start | bytes 11796484
  125.1 21.0 %all-to-all-start.3 = ((bf16[32,1,20]{2,1,0:T(2,128)(2,1)}), bf16[32,1,20]{2,1,0:T(2,128)(2,1)S(1)}, u32[]{:S(2)}, u32[]{:S(2)}) async-start(bf16[32,1,20]{2,1,0:T(2,128)(2,1)} %convert_element_type.97), calls=%async_computation.3 | async-start | bytes 32768 | tf_op jit(solution)/shard_map/all_to_all | solution.py:99
  129.1 9.0 %copy-start.9 = (f32[640,1536]{1,0:T(8,128)S(1)}, f32[640,1536]{1,0:T(8,128)}, u32[]{:S(2)}) copy-start(f32[640,1536]{1,0:T(8,128)} %copy-done.8) | copy-start | bytes 11796484
  129.2 9.0 %copy-start.11 = (f32[640,1536]{1,0:T(8,128)S(1)}, f32[640,1536]{1,0:T(8,128)}, u32[]{:S(2)}) copy-start(f32[640,1536]{1,0:T(8,128)} %get-tuple-element.12) | copy-start | bytes 11796484
  146.1 38.9 %all-to-all-start.2 = ((bf16[32,20,1536]{2,1,0:T(8,128)(2,1)}), bf16[32,20,1536]{2,1,0:T(8,128)(2,1)S(1)}, u32[]{:S(2)}, u32[]{:S(2)}) async-start(bf16[32,20,1536]{2,1,0:T(8,128)(2,1)} %reshape.96), calls=%async_computation.2 | async-start | bytes 4718592 | tf_op jit(solution)/shard_map/all_to_all | solution.py:99
  153.5 44.5 %collective-permute-start.1 = (bf16[640,1536]{1,0:T(8,128)(2,1)}, bf16[640,1536]{1,0:T(8,128)(2,1)}, u32[]{:S(2)}, u32[]{:S(2)}) collective-permute-start(bf16[640,1536]{1,0:T(8,128)(2,1)} %reshape.93), channel_id=1, source_target_pairs={{0,3},{1,0},{2,1},{3,2},{4,7},{5,4},{6,5},{7,6},{8,11},{9,8},{10,9... | collective-permute-start | bytes 5898248 | tf_op jit(solution)/shard_map/ppermute | solution.py:23
  178.6 45.4 %collective-permute-start.2 = (bf16[640,1536]{1,0:T(8,128)(2,1)}, bf16[640,1536]{1,0:T(8,128)(2,1)}, u32[]{:S(2)}, u32[]{:S(2)}) collective-permute-start(bf16[640,1536]{1,0:T(8,128)(2,1)} %collective-permute-done), channel_id=1, source_target_pairs={{0,1},{1,2},{2,3},{3,0},{4,5},{5,6},{6,7},{7,4},{8,9},{9,10},{10,1... | collective-permute-start | bytes 5898248 | tf_op jit(solution)/shard_map/ppermute | solution.py:18
  178.6 3.6 %copy-start.4 = (bf16[640,1536]{1,0:T(8,128)(2,1)S(1)}, bf16[640,1536]{1,0:T(8,128)(2,1)}, u32[]{:S(2)}) copy-start(bf16[640,1536]{1,0:T(8,128)(2,1)} %reshape.93) | copy-start | bytes 5898244
  182.2 1.7 copy-start.5
  236.8 7.8 %copy-start.6 = (bf16[2560,1536]{1,0:T(8,128)(2,1)S(1)}, bf16[2560,1536]{1,0:T(8,128)(2,1)}, u32[]{:S(2)}) copy-start(bf16[2560,1536]{1,0:T(8,128)(2,1)} %all-gather.2.cloned.1.call-done) | copy-start | bytes 23592964
  250.1 7.9 %copy-start.7 = (f32[2560,384]{1,0:T(8,128)S(1)}, f32[2560,384]{1,0:T(8,128)}, u32[]{:S(2)}) copy-start(f32[2560,384]{1,0:T(8,128)} %fusion.28) | copy-start | bytes 11796484
  262.6 4.4 %copy-start.1 = (bf16[128,1536]{1,0:T(8,128)(2,1)S(1)}, bf16[128,1536]{1,0:T(8,128)(2,1)}, u32[]{:S(2)}) copy-start(bf16[128,1536]{1,0:T(8,128)(2,1)} %param.10) | copy-start | bytes 1179652
Sparse Core Ops, SparseCore 0:
  59.5 102.8 all-gather.1
